TPU v7x, 8 devices: a whole 2x2x1 slice. The times are simulated.
8 devices in a mesh: rep: 1 (over z), dp: 8 (over x, y, core).
Axes of the slice: x: 2, y: 2, z: 1, core: 2. Of those that a mesh axis runs over, the one named last changes fastest.
Arguments:
- x: bfloat16 [8, 2048, 1280], P(('rep', 'dp'))
- dy: bfloat16 [8, 2048, 1280], P(('rep', 'dp'))
- w_gate: bfloat16 [2, 1280, 4480], replicated
- w_up: bfloat16 [2, 1280, 4480], replicated
- w_down: bfloat16 [2, 4480, 1280], replicated
- m_w_gate: float32 [2, 1280, 4480], P(None, 'dp')
- m_w_up: float32 [2, 1280, 4480], P(None, 'dp')
- m_w_down: float32 [2, 4480, 1280], P(None, 'dp')
- v_w_gate: float32 [2, 1280, 4480], P(None, 'dp')
- v_w_up: float32 [2, 1280, 4480], P(None, 'dp')
- v_w_down: float32 [2, 4480, 1280], P(None, 'dp')
Outputs:
- output 1: bfloat16 [2, 1280, 4480], P('rep')
- output 2: bfloat16 [2, 1280, 4480], P('rep')
- output 3: bfloat16 [2, 4480, 1280], P('rep')
- output 4: float32 [2, 1280, 4480], P('rep', 'dp')
- output 5: float32 [2, 1280, 4480], P('rep', 'dp')
- output 6: float32 [2, 4480, 1280], P('rep', 'dp')
- output 7: float32 [2, 1280, 4480], P('rep', 'dp')
- output 8: float32 [2, 1280, 4480], P('rep', 'dp')
- output 9: float32 [2, 4480, 1280], P('rep', 'dp')
All inputs are finite; a program needn't handle non-finite values.
Results may differ from a plain program's by a relative error of at most 0.022.
Values are sent between devices in bfloat16 or wider.
A program may use at most 2 GiB of HBM per device.

v0:
```python
import jax
import jax.numpy as jnp
from jax import lax

NAMES = ("w_gate", "w_up", "w_down")


def matmul(a, w):
    return jnp.dot(a, w, preferred_element_type=jnp.float32).astype(jnp.bfloat16)


def normed(h):
    wide = h.astype(jnp.float32)
    scale = lax.rsqrt(jnp.mean(wide**2, -1, keepdims=True) + 1e-6)
    return (wide * scale).astype(jnp.bfloat16)


def layer(h, w):
    a = normed(h)
    gate = jnp.dot(a, w["w_gate"], preferred_element_type=jnp.float32)
    up = jnp.dot(a, w["w_up"], preferred_element_type=jnp.float32)
    return h + matmul((jax.nn.silu(gate) * up).astype(jnp.bfloat16), w["w_down"])


def adamw(w, m, v, g):
    m = 0.9 * m + 0.1 * g
    v = 0.95 * v + 0.05 * g * g
    step = m * lax.rsqrt(v + 1e-8) + 0.1 * w
    return (w - 0.02 * step).astype(jnp.bfloat16), m, v


def clipped(gradients, sum_of_squares, count):
    factor = jnp.minimum(1.0, 0.5 * lax.rsqrt(sum_of_squares / count + 1e-30))
    return [g * factor for g in gradients]


def stack(weights, h):
    for number in range(weights["w_gate"].shape[0]):
        h = layer(h, {name: w[number] for name, w in weights.items()})
    return h


def solution(mesh):
    groups = mesh.shape["rep"]

    def step(x, dy, *arrays):
        weights, m, v = (arrays[i : i + 3] for i in (0, 3, 6))
        x, dy = (t.reshape(groups, -1, *t.shape[1:]) for t in (x, dy))

        def of_a_group(x, dy):
            _, back = jax.vjp(lambda w: stack(w, x), dict(zip(NAMES, weights, strict=True)))
            by_weights = back(dy)[0]
            gradients = [by_weights[name].astype(jnp.float32) for name in NAMES]
            gradients = clipped(gradients, sum(jnp.sum(g * g) for g in gradients), sum(g.size for g in gradients))
            new = [adamw(w.astype(jnp.float32), m, v, g) for w, m, v, g in zip(weights, m, v, gradients, strict=True)]
            return tuple(one[which] for which in range(3) for one in new)

        return tuple(t.reshape(-1, *t.shape[2:]) for t in jax.vmap(of_a_group)(x, dy))

    return step
```

profile of v0, /device:TPU:0, one launch (start us, length us, event | category | flops | bytes accessed | tf_op | source)
XLA Modules:
  0.0 1664.8 jit_solution(14344349423737793933)
XLA Ops:
  7.2 0.0 reduce-scatter.29.cloned.1.call-start
  7.2 3.6 fusion.53
  10.8 8.0 copy
  18.8 32.1 %fusion.47 = f32[2048,4480]{1,0:T(8,128)} fusion(bf16[2,1280,4480]{2,1,0:T(8,128)(2,1)} %param, bf16[1,2048,1280]{2,1,0:T(8,128)(2,1)} %param.4, f32[2048]{0:T(1024)S(1)} %add_rsqrt_fusion), kind=kOutput, calls=%fused_computation.64 | convolution fusion | flops 23495966720 | bytes 53420032 | tf_op jit(solution)/vmap(jvp())/dot_general | solution.py:20
  51.0 30.1 %fusion.45 = f32[2048,4480]{1,0:T(8,128)} fusion(bf16[2,1280,4480]{2,1,0:T(8,128)(2,1)} %param.5, bf16[1,2048,1280]{2,1,0:T(8,128)(2,1)S(1)} %bitcast.360, f32[2048]{0:T(1024)S(1)} %add_rsqrt_fusion), kind=kOutput, calls=%fused_computation.62 | convolution fusion | flops 23495966720 | bytes 53420032 | tf_op jit(solution)/vmap(jvp())/dot_general | solution.py:21
  81.0 30.6 %fusion.26 = bf16[2048,4480]{1,0:T(8,128)(2,1)} fusion(f32[2048,4480]{1,0:T(8,128)} %fusion.45, f32[2048,4480]{1,0:T(8,128)} %fusion.47), kind=kLoop, calls=%fused_computation.37 | loop fusion | flops 55050240 | bytes 91750400
  111.6 33.2 %fusion.57 = (f32[2048]{0:T(1024)S(1)}, bf16[1,2048,1280]{1,2,0:T(8,128)(2,1)}) fusion(bf16[1,2048,1280]{1,2,0:T(8,128)(2,1)} %copy, bf16[2048,4480]{1,0:T(8,128)(2,1)} %fusion.26, bf16[2,4480,1280]{2,1,0:T(8,128)(2,1)} %param.3), kind=kOutput, calls=%fused_computation.74 | convolution fusion | flops 23501207552 | bytes 40312832 | tf_op jit(solution)/vmap(jvp())/dot_general | solution.py:9
  144.9 0.6 copy-done.5
  145.4 32.1 %fusion.35 = f32[2048,4480]{1,0:T(8,128)} fusion(bf16[2,1280,4480]{2,1,0:T(8,128)(2,1)} %param, bf16[1,2048,1280]{1,2,0:T(8,128)(2,1)} %get-tuple-element.10, f32[2048]{0:T(1024)S(1)} %bitcast.366), kind=kOutput, calls=%fused_computation.52 | convolution fusion | flops 23495966720 | bytes 53420032 | tf_op jit(solution)/vmap(jvp())/dot_general | solution.py:20
  177.6 31.1 %fusion.39 = f32[2048,4480]{1,0:T(8,128)} fusion(bf16[2,1280,4480]{2,1,0:T(8,128)(2,1)} %param.5, bf16[1,2048,1280]{1,2,0:T(8,128)(2,1)S(1)} %copy-done.4, f32[2048]{0:T(1024)S(1)} %bitcast.367), kind=kOutput, calls=%fused_computation.56 | convolution fusion | flops 23495966720 | bytes 53420032 | tf_op jit(solution)/vmap(jvp())/dot_general | solution.py:21
  208.7 30.5 %convolution_convert_fusion.1 = bf16[2048,4480]{1,0:T(8,128)(2,1)} fusion(bf16[2,4480,1280]{2,1,0:T(8,128)(2,1)} %param.3, bf16[1,2048,1280]{2,1,0:T(8,128)(2,1)S(1)} %bitcast.362), kind=kOutput, calls=%fused_computation.36 | convolution fusion | flops 23497277440 | bytes 35061760 | tf_op jit(solution)/vmap(transpose(jvp()))/dot_general | solution.py:9
  239.2 7.9 copy.1
  247.1 36.0 %fusion.6 = bf16[2048,4480]{1,0:T(8,128)(2,1)} fusion(f32[2048,4480]{1,0:T(8,128)} %fusion.35, f32[2048,4480]{1,0:T(8,128)} %fusion.39, bf16[2048,4480]{1,0:T(8,128)(2,1)} %convolution_convert_fusion.1), kind=kLoop, calls=%fused_computation.11 | loop fusion | flops 110100480 | bytes 110100480
  283.1 32.0 %fusion.71 = bf16[2048,1280]{0,1:T(8,128)(2,1)} fusion(bf16[2048,4480]{1,0:T(8,128)(2,1)} %fusion.6, bf16[2,1280,4480]{2,1,0:T(8,128)(2,1)} %param), kind=kOutput, calls=%fused_computation.87 | convolution fusion | flops 23488102400 | bytes 35061760 | tf_op jit(solution)/vmap(transpose(jvp()))/dot_general | solution.py:20
  315.0 36.9 %fusion.59 = (f32[2048]{0:T(1024)S(1)}, bf16[1,2048,1280]{1,2,0:T(8,128)(2,1)}) fusion(bf16[1,2048,1280]{1,2,0:T(8,128)(2,1)} %get-tuple-element.10, bf16[2048,1280]{0,1:T(8,128)(2,1)} %fusion.71, bf16[2,1280,4480]{2,1,0:T(8,128)(2,1)} %param.5, bf16[2048,4480]{1,0:T(8,128)(2,1)} %convolution_convert_fusion.1, f32[2048,4480]{1,0:T(8,128)} %fusion.35), kind=kOutput, calls=%fused_computation.76 | convolution fusion | flops 23558879232 | bytes 82255872 | tf_op jit(solution)/vmap(transpose(jvp()))/dot_general | solution.py:21
  352.0 12.4 fusion.122
  364.4 30.7 %fusion.146 = f32[1280,4480]{0,1:T(8,128)} fusion(bf16[2048,1280]{0,1:T(8,128)(2,1)} %fusion.122, bf16[2048,4480]{1,0:T(8,128)(2,1)} %fusion.26), kind=kOutput, calls=%fused_computation.162 | convolution fusion | flops 23488102400 | bytes 46530560 | tf_op jit(solution)/vmap(transpose(jvp()))/dot_general | solution.py:9
  395.1 0.0 reduce-scatter.29.cloned.1.call-update
  395.2 0.0 reduce-scatter.27.cloned.1.call-start
  395.2 41.3 %fusion.28 = f32[4480,1280]{1,0:T(8,128)} fusion(f32[2048,4480]{1,0:T(8,128)} %fusion.39, f32[2048,4480]{1,0:T(8,128)} %fusion.35, bf16[1,2048,1280]{2,1,0:T(8,128)(2,1)} %param.2), kind=kOutput, calls=%fused_computation.39 | convolution fusion | flops 23543152640 | bytes 101580800 | tf_op jit(solution)/vmap(transpose(jvp()))/dot_general | solution.py:9
  436.5 0.0 reduce-scatter.27.cloned.1.call-update
  436.6 0.0 reduce-scatter.25.cloned.1.call-start
  436.6 32.0 %convolution_convert_fusion = bf16[2048,4480]{1,0:T(8,128)(2,1)} fusion(bf16[2048,1280]{0,1:T(8,128)(2,1)} %fusion.122, bf16[2,4480,1280]{2,1,0:T(8,128)(2,1)} %param.3), kind=kOutput, calls=%fused_computation.35 | convolution fusion | flops 23497277440 | bytes 35061760 | tf_op jit(solution)/vmap(transpose(jvp()))/dot_general | solution.py:9
  468.6 39.0 %fusion.2 = f32[4480,1280]{0,1:T(8,128)} fusion(bf16[2048,4480]{1,0:T(8,128)(2,1)} %convolution_convert_fusion, f32[2048,4480]{1,0:T(8,128)} %fusion.47, bf16[1,2048,1280]{2,1,0:T(8,128)(2,1)} %param.4, f32[2048]{0:T(1024)S(1)} %copy-done.11), kind=kOutput, calls=%fused_computation.8 | convolution fusion | flops 23551016960 | bytes 83238912 | tf_op jit(solution)/vmap(transpose(jvp()))/dot_general | solution.py:21
  507.7 0.0 reduce-scatter.25.cloned.1.call-update
  507.7 0.0 reduce-scatter.23.cloned.1.call-start
  507.8 0.6 copy-done.9
  508.4 38.0 %fusion.22 = f32[4480,1280]{0,1:T(8,128)} fusion(bf16[2048,4480]{1,0:T(8,128)(2,1)} %convolution_convert_fusion.1, f32[2048,4480]{1,0:T(8,128)} %fusion.35, bf16[1,2048,1280]{1,2,0:T(8,128)(2,1)} %get-tuple-element.10, f32[2048]{0:T(1024)S(1)} %bitcast.369), kind=kOutput, calls=%fused_computation.33 | convolution fusion | flops 23551016960 | bytes 83238912 | tf_op jit(solution)/vmap(transpose(jvp()))/dot_general | solution.py:21
  546.4 0.0 reduce-scatter.23.cloned.1.call-update
  546.4 0.0 reduce-scatter.21.cloned.1.call-start
  546.5 47.4 %fusion.10 = f32[4480,1280]{0,1:T(8,128)} fusion(f32[2048,4480]{1,0:T(8,128)} %fusion.47, f32[2048,4480]{1,0:T(8,128)} %fusion.45, bf16[2048,4480]{1,0:T(8,128)(2,1)} %convolution_convert_fusion, bf16[1,2048,1280]{2,1,0:T(8,128)(2,1)} %param.4, f32[2048]{0:T(1024)S(1)} %copy-done.11), kind=kOutput, calls=%fused_computation.15 | convolution fusion | flops 23596892160 | bytes 119939072 | tf_op jit(solution)/vmap(transpose(jvp()))/dot_general | solution.py:20
  593.9 0.0 reduce-scatter.19.cloned.1.call-start
  594.0 30.8 %fusion.127 = f32[4480,1280]{0,1:T(8,128)} fusion(bf16[2048,4480]{1,0:T(8,128)(2,1)} %fusion.6, bf16[1,2048,1280]{1,2,0:T(8,128)(2,1)} %get-tuple-element.10, f32[2048]{0:T(1024)S(1)} %bitcast.370), kind=kOutput, calls=%fused_computation.138 | convolution fusion | flops 23495966720 | bytes 46538752 | tf_op jit(solution)/vmap(transpose(jvp()))/dot_general | solution.py:20
  624.8 0.5 all-gather.14.cloned.1.call-start
  625.3 0.0 reduce-scatter.29.cloned.1.call-done
  625.3 2.0 convert_bitcast_fusion.3
  627.3 46.6 %reduce-scatter.27.cloned.1.call-done = f32[560,1280]{1,0:T(8,128)} async-done(((f32[4480,1280]{1,0:T(8,128)}), f32[560,1280]{1,0:T(8,128)}) %reduce-scatter.27.cloned.1.call-update) | async-done | bytes 2867216
  674.0 2.0 convert_bitcast_fusion.4
  675.9 1.1 copy-done.3
  677.0 2.1 fusion.106
  679.1 135.2 %reduce-scatter.25.cloned.1.call-done = f32[4480,160]{0,1:T(8,128)} async-done(((f32[4480,1280]{0,1:T(8,128)}), f32[4480,160]{0,1:T(8,128)}) %reduce-scatter.25.cloned.1.call-update) | async-done | bytes 2867216
  814.3 2.0 convert_bitcast_fusion.5
  816.2 137.6 %reduce-scatter.23.cloned.1.call-done = f32[4480,160]{0,1:T(8,128)} async-done(((f32[4480,1280]{0,1:T(8,128)}), f32[4480,160]{0,1:T(8,128)}) %reduce-scatter.23.cloned.1.call-update) | async-done | bytes 2867216
  953.9 2.0 convert_bitcast_fusion.6
  955.8 1.1 copy-done.1
  956.9 2.1 fusion.105
  959.0 135.0 %reduce-scatter.21.cloned.1.call-done = f32[4480,160]{0,1:T(8,128)} async-done(((f32[4480,1280]{0,1:T(8,128)}), f32[4480,160]{0,1:T(8,128)}) %reduce-scatter.21.cloned.1.call-update) | async-done | bytes 2867216
  1094.0 2.0 convert_bitcast_fusion.7
  1095.9 138.2 %reduce-scatter.19.cloned.1.call-done = f32[4480,160]{0,1:T(8,128)} async-done(((f32[4480,1280]{0,1:T(8,128)}), f32[4480,160]{0,1:T(8,128)}) %reduce-scatter.19.cloned.1.call-update) | async-done | bytes 2867216
  1234.1 2.0 convert_bitcast_fusion.8
  1236.1 1.1 copy-done
  1237.2 2.1 fusion.104
  1241.2 22.2 %all-reduce.16 = f32[]{:T(128)} all-reduce(f32[]{:T(128)S(6)} %add.114), channel_id=5, replica_groups=mesh['rep'=1,'dp'=8] {'dp'}, use_global_device_ids=true, to_apply=%region_3.4.clone | all-reduce | flops 1 | bytes 8 | tf_op jit(solution)/vmap()/reduce_sum | solution.py:54
  1264.2 10.5 fusion.136
  1274.7 0.0 all-gather.12.cloned.1.call-start
  1274.7 10.1 fusion.134
  1284.9 0.0 all-gather.10.cloned.1.call-start
  1284.9 10.1 fusion.135
  1295.0 91.9 %all-gather.14.cloned.1.call-done = bf16[1,2,4480,1280]{3,2,1,0:T(8,128)(2,1)} async-done(((bf16[1,2,560,1280]{3,2,1,0:T(8,128)(2,1)}), bf16[1,2,4480,1280]{3,2,1,0:T(8,128)(2,1)}) %all-gather.14.cloned.1.call-update) | async-done | bytes 22937616 | tf_op jit(solution)/reshape | solution.py:58
  1386.9 112.6 %all-gather.12.cloned.1.call-done = bf16[1,2,1280,4480]{3,2,1,0:T(8,128)(2,1)} async-done(((bf16[1,2,160,4480]{3,2,1,0:T(8,128)(2,1)}), bf16[1,2,1280,4480]{3,2,1,0:T(8,128)(2,1)}) %all-gather.12.cloned.1.call-update) | async-done | bytes 22937616 | tf_op jit(solution)/reshape | solution.py:58
  1499.6 112.6 %all-gather.10.cloned.1.call-done = bf16[1,2,1280,4480]{3,2,1,0:T(8,128)(2,1)} async-done(((bf16[1,2,160,4480]{3,2,1,0:T(8,128)(2,1)}), bf16[1,2,1280,4480]{3,2,1,0:T(8,128)(2,1)}) %all-gather.10.cloned.1.call-update) | async-done | bytes 22937616 | tf_op jit(solution)/reshape | solution.py:58
  1612.2 19.0 %copy.5 = bf16[2,1280,4480]{2,1,0:T(8,128)(2,1)} copy(bf16[2,1280,4480]{2,1,0:T(8,128)(2,1)} %bitcast.358) | data formatting | bytes 45875200
  1631.2 18.7 %copy.6 = bf16[2,1280,4480]{2,1,0:T(8,128)(2,1)} copy(bf16[2,1280,4480]{2,1,0:T(8,128)(2,1)} %bitcast.357) | data formatting | bytes 45875200
  1649.9 8.2 copy.7
  (51 shorter events, 0.2 us)
Async XLA Ops:
  7.2 618.2 %reduce-scatter.29.cloned.1.call-start = ((), (), s32[]{:S(2)}) async-start(), calls=%async_computation.14 | async-start | bytes 25804800
  10.8 40.2 %slice-start.6 = ((s8[5242880]{0:T(1024)(128)(4,1)}), s8[1048576]{0:T(1024)(128)(4,1)S(1)}, s32[]{:S(2)}) async-start(s8[5242880]{0:T(1024)(128)(4,1)} %bitcast.359), calls=%async_computation.21 | async-start | bytes 2097152
  18.8 32.2 %copy-start.10 = (f32[2048]{0:T(1024)}, f32[2048]{0:T(1024)S(1)}, u32[]{:S(2)}) copy-start(f32[2048]{0:T(1024)S(1)} %add_rsqrt_fusion) | copy-start | bytes 24580
  18.8 32.2 %slice-start.7 = ((s8[5242880]{0:T(1024)(128)(4,1)}), s8[4194304]{0:T(1024)(128)(4,1)S(1)}, s32[]{:S(2)}) async-start(s8[5242880]{0:T(1024)(128)(4,1)} %bitcast.359), calls=%async_computation.22 | async-start | bytes 8388608
  144.8 0.6 copy-start.5
  144.9 32.7 %copy-start.7 = (f32[1,2048]{1,0:T(1,128)}, f32[1,2048]{1,0:T(1,128)S(1)}, u32[]{:S(2)}) copy-start(f32[1,2048]{1,0:T(1,128)S(1)} %rsqrt.32) | copy-start | bytes 24580
  145.4 32.1 %copy-start.4 = (bf16[1,2048,1280]{1,2,0:T(8,128)(2,1)S(1)}, bf16[1,2048,1280]{1,2,0:T(8,128)(2,1)}, u32[]{:S(2)}) copy-start(bf16[1,2048,1280]{1,2,0:T(8,128)(2,1)} %get-tuple-element.10) | copy-start | bytes 15728644
  145.4 63.2 %slice-start.8 = ((s8[5242880]{0:T(1024)(128)(4,1)}), s8[4194304]{0:T(1024)(128)(4,1)S(1)}, s32[]{:S(2)}) async-start(s8[5242880]{0:T(1024)(128)(4,1)} %bitcast.361), calls=%async_computation.23 | async-start | bytes 8388608
  177.6 31.1 %slice-start.9 = ((s8[5242880]{0:T(1024)(128)(4,1)}), s8[1048576]{0:T(1024)(128)(4,1)S(1)}, s32[]{:S(2)}) async-start(s8[5242880]{0:T(1024)(128)(4,1)} %bitcast.361), calls=%async_computation.24 | async-start | bytes 2097152
  315.0 36.9 %copy-start.6 = (f32[2048]{0:T(1024)S(1)}, f32[2048]{0:T(1024)}, u32[]{:S(2)}) copy-start(f32[2048]{0:T(1024)} %copy-done.5) | copy-start | bytes 24580
  315.0 37.0 %copy-start.8 = (f32[1,2048]{1,0:T(1,128)S(1)}, f32[1,2048]{1,0:T(1,128)}, u32[]{:S(2)}) copy-start(f32[1,2048]{1,0:T(1,128)} %copy-done.7) | copy-start | bytes 24580
  395.2 278.8 %reduce-scatter.27.cloned.1.call-start = ((), (), s32[]{:S(2)}) async-start(), calls=%async_computation.13 | async-start | bytes 25804800
  436.5 32.1 %copy-start.11 = (f32[2048]{0:T(1024)S(1)}, f32[2048]{0:T(1024)}, u32[]{:S(2)}) copy-start(f32[2048]{0:T(1024)} %copy-done.10) | copy-start | bytes 24580
  436.6 377.7 %reduce-scatter.25.cloned.1.call-start = ((), (), s32[]{:S(2)}) async-start(), calls=%async_computation.12 | async-start | bytes 25804800
  507.7 0.7 copy-start.9
  507.7 446.1 %reduce-scatter.23.cloned.1.call-start = ((), (), s32[]{:S(2)}) async-start(), calls=%async_computation.11 | async-start | bytes 25804800
  546.4 547.6 %reduce-scatter.21.cloned.1.call-start = ((), (), s32[]{:S(2)}) async-start(), calls=%async_computation.10 | async-start | bytes 25804800
  593.9 640.2 %reduce-scatter.19.cloned.1.call-start = ((), (), s32[]{:S(2)}) async-start(), calls=%async_computation.9 | async-start | bytes 25804800
  624.8 762.1 %all-gather.14.cloned.1.call-start = ((), (), s32[]{:S(2)}) async-start(), calls=%async_computation.8 | async-start | bytes 25804800 | tf_op jit(solution)/reshape | solution.py:58
  627.3 188.9 %copy-start.2 = (bf16[1,1,560,1280]{3,2,1,0:T(8,128)(2,1)}, bf16[1,1,560,1280]{3,2,1,0:T(8,128)(2,1)S(1)}, u32[]{:S(2)}) copy-start(bf16[1,1,560,1280]{3,2,1,0:T(8,128)(2,1)S(1)} %convert_bitcast_fusion.3) | copy-start | bytes 4300804
  675.9 1.1 copy-start.3
  955.8 1.1 copy-start.1
  1236.1 1.1 copy-start
  1274.7 224.9 %all-gather.12.cloned.1.call-start = ((), (), s32[]{:S(2)}) async-start(), calls=%async_computation.7 | async-start | bytes 25804800 | tf_op jit(solution)/reshape | solution.py:58
  1284.9 327.4 %all-gather.10.cloned.1.call-start = ((), (), s32[]{:S(2)}) async-start(), calls=%async_computation.6 | async-start | bytes 25804800 | tf_op jit(solution)/reshape | solution.py:58
  1612.2 37.7 %slice-start = ((s8[22937600]{0:T(1024)(128)(4,1)}), s8[4194304]{0:T(1024)(128)(4,1)S(1)}, s32[]{:S(2)}) async-start(s8[22937600]{0:T(1024)(128)(4,1)} %bitcast.354), calls=%async_computation.15 | async-start | bytes 8388608
  1612.2 37.7 %slice-start.1 = ((s8[22937600]{0:T(1024)(128)(4,1)}), s8[4194304]{0:T(1024)(128)(4,1)S(1)}, s32[]{:S(2)}) async-start(s8[22937600]{0:T(1024)(128)(4,1)} %bitcast.354), calls=%async_computation.16 | async-start | bytes 8388608
  1612.2 37.7 %slice-start.2 = ((s8[22937600]{0:T(1024)(128)(4,1)}), s8[4194304]{0:T(1024)(128)(4,1)S(1)}, s32[]{:S(2)}) async-start(s8[22937600]{0:T(1024)(128)(4,1)} %bitcast.354), calls=%async_computation.17 | async-start | bytes 8388608
  1631.2 18.7 %slice-start.3 = ((s8[22937600]{0:T(1024)(128)(4,1)}), s8[4194304]{0:T(1024)(128)(4,1)S(1)}, s32[]{:S(2)}) async-start(s8[22937600]{0:T(1024)(128)(4,1)} %bitcast.354), calls=%async_computation.18 | async-start | bytes 8388608
  1631.2 18.7 %slice-start.4 = ((s8[22937600]{0:T(1024)(128)(4,1)}), s8[4194304]{0:T(1024)(128)(4,1)S(1)}, s32[]{:S(2)}) async-start(s8[22937600]{0:T(1024)(128)(4,1)} %bitcast.354), calls=%async_computation.19 | async-start | bytes 8388608
  1631.2 18.7 %slice-start.5 = ((s8[22937600]{0:T(1024)(128)(4,1)}), s8[1966080]{0:T(1024)(128)(4,1)S(1)}, s32[]{:S(2)}) async-start(s8[22937600]{0:T(1024)(128)(4,1)} %bitcast.354), calls=%async_computation.20 | async-start | bytes 3932160
Sparse Core Ops, SparseCore 0:
  395.3 138.9 reduce-scatter.28
  537.8 136.1 reduce-scatter.26
  678.1 136.1 reduce-scatter.24
  817.7 136.1 reduce-scatter.22
  957.8 136.1 reduce-scatter.20
  1098.0 136.1 reduce-scatter.18
  1274.8 112.0 all-gather.13
  1389.3 110.1 all-gather.11
  1502.0 110.1 all-gather.9
where the time goes:
time: 1670 us; the launch traced here: 1660 us
  waiting for transfers between devices  910 us (54%)
  matrix products  517 us (31%)
  other arithmetic  131 us (8%)
  local copies, waits for them, and re-layouts  66.3 us (4%)
  blocking collectives  22.2 us (1%)
  between operations  16.9 us (1%)
    unnamed x15, waiting for transfers between devices  593 us
    reshape x3, waiting for transfers between devices, step(): t.reshape(-1, *t.shape[2:])  317 us
    dot_general x5, matrix products, layer(): up = jnp.dot(a, w['w_up'], preferred_element_type=jnp.float32)  175 us
    dot_general x5, matrix products, layer(): gate = jnp.dot(a, w['w_gate'], preferred_element_type=jnp.float32)  174 us
    dot_general x5, matrix products, matmul(): jnp.dot(a, w, preferred_element_type=jnp.float32).astype(jnp.bfloat16)  168 us
    unnamed x6, other arithmetic  79 us
    unnamed x49, local copies, waits for them, and re-layouts  66.2 us
  transfers between devices with their start and end apart: 9, of which 8 were waited for; matrix products, arithmetic and copies ran while one was open for 16% of the time, Pallas kernels for 0%

commit v1 on v0

v1 whole, which is shorter than its diff:
```python
import jax
import jax.numpy as jnp
from jax import lax
from jax.sharding import PartitionSpec as P

F32, BF16 = jnp.float32, jnp.bfloat16


def dot(a, b, dims):
    return lax.dot_general(a, b, (dims, ((), ())), preferred_element_type=F32)


def scale_of(h):
    wide = h.astype(F32)
    return wide, lax.rsqrt(jnp.mean(wide**2, -1, keepdims=True) + 1e-6)


def forward(h, wg, wu):
    wide, scale = scale_of(h)
    a = (wide * scale).astype(BF16)
    gate, up = dot(a, wg, ((1,), (0,))), dot(a, wu, ((1,), (0,)))
    return a, gate, up, (jax.nn.silu(gate) * up).astype(BF16)


def hidden_back(d_act, gate, up):
    d = d_act.astype(F32)
    s = jax.nn.sigmoid(gate)
    d_up = d * (gate * s)
    d_gate = d * up * (s * (1.0 + gate * (1.0 - s)))
    return d_gate.astype(BF16), d_up.astype(BF16)


def norm_back(h, da, dh):
    wide, scale = scale_of(h)
    da = da.astype(F32)
    along = jnp.sum(da * wide, -1, keepdims=True)
    d_wide = da * scale - wide * (along * scale**3 / h.shape[-1])
    return dh + d_wide.astype(BF16)


def adamw(w, m, v, g):
    m = 0.9 * m + 0.1 * g
    v = 0.95 * v + 0.05 * g * g
    step = m * lax.rsqrt(v + 1e-8) + 0.1 * w
    return (w - 0.02 * step).astype(BF16), m, v


def solution(mesh):
    n = mesh.shape["dp"]

    def scatter(g):
        return lax.psum_scatter(g.astype(BF16), "dp", scatter_dimension=0, tiled=True)

    def device_step(x, dy, wg, wu, wd, mg, mu, md, vg, vu, vd):
        x, dy = x[0], dy[0]
        T, N, M = ((0,), (0,)), ((1,), (0,)), ((1,), (1,))
        a0, gate0, up0, act0 = forward(x, wg[0], wu[0])
        h1 = x + dot(act0, wd[0], N).astype(BF16)
        a1, gate1, up1, act1 = forward(h1, wg[1], wu[1])
        gd1 = scatter(dot(act1, dy, T))
        dact1 = dot(dy, wd[1], M).astype(BF16)
        dgate1, dup1 = hidden_back(dact1, gate1, up1)
        gg1 = scatter(dot(a1, dgate1, T))
        gu1 = scatter(dot(a1, dup1, T))
        da1 = dot(dgate1, wg[1], M).astype(BF16) + dot(dup1, wu[1], M).astype(BF16)
        dh1 = norm_back(h1, da1, dy)
        gd0 = scatter(dot(act0, dh1, T))
        dact0 = dot(dh1, wd[0], M).astype(BF16)
        dgate0, dup0 = hidden_back(dact0, gate0, up0)
        gg0 = scatter(dot(a0, dgate0, T))
        gu0 = scatter(dot(a0, dup0, T))
        grads = ((gg0, gg1), (gu0, gu1), (gd0, gd1))
        squares = sum(jnp.sum(jnp.square(g.astype(F32))) for pair in grads for g in pair)
        count = sum(g.size for pair in grads for g in pair) * n
        total = lax.psum(squares, "dp")
        factor = jnp.minimum(1.0, 0.5 * lax.rsqrt(total / count + 1e-30))
        me = lax.axis_index("dp")
        ws, ms, vs = [], [], []
        for pair, w, m, v in zip(grads, (wg, wu, wd), (mg, mu, md), (vg, vu, vd)):
            rows = m.shape[1]
            new = []
            for l in range(2):
                own = lax.dynamic_slice_in_dim(w[l], me * rows, rows, 0).astype(F32)
                new.append(adamw(own, m[l], v[l], pair[l].astype(F32) * factor))
            ws.append(jnp.stack([lax.all_gather(new[l][0], "dp", axis=0, tiled=True) for l in range(2)]))
            ms.append(jnp.stack([new[l][1] for l in range(2)]))
            vs.append(jnp.stack([new[l][2] for l in range(2)]))
        return (*ws, *ms, *vs)

    tokens, whole, rows = P(("rep", "dp"), None, None), P(None, None, None), P(None, "dp", None)
    return jax.shard_map(
        device_step,
        mesh=mesh,
        in_specs=(tokens,) * 2 + (whole,) * 3 + (rows,) * 6,
        out_specs=(P("rep", None, None),) * 3 + (P("rep", "dp", None),) * 6,
        check_vma=False,
    )
```

time: 1670 us -> 1310 us (0.78)
  waiting for transfers between devices: 910 us -> 512 us
  matrix products: 517 us -> 555 us
    unnamed x15 -> x12, waiting for transfers between devices: 593 us -> 1.9 us
    reshape x3 -> x0, waiting for transfers between devices: 317 us -> none  [step(): t.reshape(-1, *t.shape[2:])]
    all_gather x0 -> x6, waiting for transfers between devices: none -> 278 us  [device_step(): lax.all_gather(new[l][0], 'dp', axis=0, tiled=True)]
    reduce_scatter x0 -> x6, waiting for transfers between devices: none -> 232 us  [scatter(): lax.psum_scatter(g.astype(BF16), 'dp', scatter_dimension=0, tiled=True)]
    another operation x0 -> x6, other arithmetic: none -> 79.4 us  [the longest x3 59.6 us: device_step(): jnp.stack([lax.all_gather(new[l][0], 'dp', axis=0, tiled=True) for l in r...]
    unnamed x6 -> x0, other arithmetic: 79 us -> none
    unnamed x49 -> x36, local copies, waits for them, and re-layouts: 66.2 us -> 21.5 us
    dot_general x15, matrix products: 517 us -> 555 us  [dot(): return lax.dot_general(a, b, (dims, ((), ())), preferred_element_type=F32)]
  transfers between devices with their start and end apart: 9 -> 12, of which waited for: 8 -> 9; matrix products, arithmetic and copies ran while one was open for 16% -> 33% of each run, Pallas kernels for 0% -> 0%
where the time goes in v1:
time: 1310 us
  matrix products  555 us (42%)
  waiting for transfers between devices  512 us (39%)
  other arithmetic  141 us (11%)
  local copies, waits for them, and re-layouts  55.4 us (4%)
  blocking collectives  22.5 us (2%)
  between operations  19.4 us (1%)
    dot_general x15, matrix products, dot(): return lax.dot_general(a, b, (dims, ((), ())), preferred_element_type=F32)  555 us
    all_gather x6, waiting for transfers between devices, device_step(): lax.all_gather(new[l][0], 'dp', axis=0, tiled=True)  278 us
    reduce_scatter x6, waiting for transfers between devices, scatter(): lax.psum_scatter(g.astype(BF16), 'dp', scatter_dimension=0, tiled=True)  232 us
    another operation x3, other arithmetic, device_step(): jnp.stack([lax.all_gather(new[l][0], 'dp', axis=0, tiled=True) for l in r...  59.6 us
    convert_element_type x3, other arithmetic, adamw(): return ((w - 0.02 * step).astype(BF16), m, v)  29.1 us
  transfers between devices with their start and end apart: 12, of which 9 were waited for; matrix products, arithmetic and copies ran while one was open for 33% of the time, Pallas kernels for 0%

profile of v1, /device:TPU:0, one launch (start us, length us, event | category | flops | bytes accessed | tf_op | source)
XLA Modules:
  0.0 1305.7 jit_solution(11359392558668113688)
XLA Ops:
  7.2 7.9 copy.20
  15.1 3.6 fusion.26
  18.7 31.6 %fusion.23 = f32[2048,4480]{1,0:T(8,128)} fusion(bf16[1,2048,1280]{2,1,0:T(8,128)(2,1)} %param.11, f32[2048]{0:T(1024)S(1)} %add_rsqrt_fusion.1, bf16[2,1280,4480]{2,1,0:T(8,128)(2,1)} %param.13), kind=kOutput, calls=%fused_computation.47 | convolution fusion | flops 23495966720 | bytes 53420032 | tf_op jit(solution)/shard_map/dot_general | solution.py:10
  50.3 45.4 %multiply_convert_fusion.1 = (bf16[2048,4480]{1,0:T(8,128)(2,1)}, f32[2048,4480]{1,0:T(8,128)}) fusion(f32[2048,4480]{1,0:T(8,128)} %fusion.23, bf16[2,1280,4480]{2,1,0:T(8,128)(2,1)} %param.14, bf16[1,2048,1280]{2,1,0:T(8,128)(2,1)} %param.11, f32[2048]{0:T(1024)S(1)} %add_rsqrt_fusion.1), kind=kOutput, calls=%fused_computation.13 | convolution fusion | flops 23551016960 | bytes 108470272 | tf_op jit(solution)/shard_map/dot_general | solution.py:10
  95.8 45.6 %fusion.30 = (f32[2048]{0:T(1024)S(1)}, bf16[2048,1280]{0,1:T(8,128)(2,1)}) fusion(bf16[2048,4480]{1,0:T(8,128)(2,1)} %get-tuple-element.35, bf16[2,4480,1280]{2,1,0:T(8,128)(2,1)} %param.15, bf16[1,2048,1280]{1,2,0:T(8,128)(2,1)} %copy.20), kind=kOutput, calls=%fused_computation.54 | convolution fusion | flops 23501207552 | bytes 40312832 | tf_op jit(solution)/shard_map/dot_general | solution.py:10
  141.4 31.5 %convolution_convert_fusion.5 = bf16[2048,4480]{1,0:T(8,128)(2,1)} fusion(bf16[1,2048,1280]{2,1,0:T(8,128)(2,1)} %param.12, bf16[2,4480,1280]{2,1,0:T(8,128)(2,1)} %param.15), kind=kOutput, calls=%fused_computation.24 | convolution fusion | flops 23497277440 | bytes 35061760 | tf_op jit(solution)/shard_map/dot_general | solution.py:10
  172.9 30.7 %fusion.12 = f32[2048,4480]{1,0:T(8,128)} fusion(bf16[2048,1280]{0,1:T(8,128)(2,1)S(1)} %copy-done.10, f32[2048]{0:T(1024)S(1)} %add_rsqrt_fusion, bf16[2,1280,4480]{2,1,0:T(8,128)(2,1)} %param.13), kind=kOutput, calls=%fused_computation.36 | convolution fusion | flops 23495966720 | bytes 53420032 | tf_op jit(solution)/shard_map/dot_general | solution.py:10
  203.6 59.3 %fusion.1 = (bf16[2048,4480]{1,0:T(8,128)(2,1)}, bf16[2048,4480]{1,0:T(8,128)(2,1)}, f32[2048,4480]{1,0:T(8,128)}) fusion(bf16[2048,4480]{1,0:T(8,128)(2,1)} %convolution_convert_fusion.5, f32[2048,4480]{1,0:T(8,128)} %fusion.12, bf16[2,1280,4480]{2,1,0:T(8,128)(2,1)} %param.14, bf16[2048,1280]{0,1:T(8,128)(2,1)} %get-tuple-element.38, ...), kind=kOutput, calls=%fused_computation.5 | convolution fusion | flops 23624417280 | bytes 145170432 | tf_op jit(solution)/shard_map/dot_general | solution.py:10
  262.9 31.2 %convolution_convert_fusion.2 = bf16[1280,4480]{1,0:T(8,128)(2,1)} fusion(bf16[2048,4480]{1,0:T(8,128)(2,1)} %get-tuple-element.9, bf16[2048,1280]{0,1:T(8,128)(2,1)} %get-tuple-element.38, f32[2048]{0:T(1024)S(1)} %add_rsqrt_fusion), kind=kOutput, calls=%fused_computation.21 | convolution fusion | flops 23501701120 | bytes 35069952 | tf_op jit(solution)/shard_map/dot_general | solution.py:10
  294.1 0.0 reduce-scatter.7.cloned.1.call-start
  294.2 32.2 %fusion.36 = bf16[2048,1280]{0,1:T(8,128)(2,1)} fusion(bf16[2048,4480]{1,0:T(8,128)(2,1)} %get-tuple-element.10, bf16[2,1280,4480]{2,1,0:T(8,128)(2,1)} %param.14), kind=kOutput, calls=%fused_computation.59 | convolution fusion | flops 23490723840 | bytes 35061760 | tf_op jit(solution)/shard_map/dot_general | solution.py:10
  326.4 34.0 %fusion.32 = (f32[2048]{0:T(1024)S(1)}, bf16[2048,1280]{0,1:T(8,128)(2,1)}) fusion(bf16[2048,1280]{0,1:T(8,128)(2,1)} %get-tuple-element.38, bf16[2048,1280]{0,1:T(8,128)(2,1)} %fusion.36, bf16[2048,4480]{1,0:T(8,128)(2,1)} %get-tuple-element.9, bf16[2,1280,4480]{2,1,0:T(8,128)(2,1)} %param.13), kind=kOutput, calls=%fused_computation.56 | convolution fusion | flops 23503828992 | bytes 45555712 | tf_op jit(solution)/shard_map/dot_general | solution.py:10
  360.3 8.1 copy.21
  368.5 12.4 fusion.51
  380.9 31.5 %convolution_convert_fusion.4 = bf16[2048,4480]{1,0:T(8,128)(2,1)} fusion(bf16[2048,1280]{0,1:T(8,128)(2,1)} %fusion.51, bf16[2,4480,1280]{2,1,0:T(8,128)(2,1)} %param.15), kind=kOutput, calls=%fused_computation.23 | convolution fusion | flops 23497277440 | bytes 35061760 | tf_op jit(solution)/shard_map/dot_general | solution.py:10
  412.4 44.0 %convolution_convert_fusion.3 = bf16[1280,4480]{1,0:T(8,128)(2,1)} fusion(f32[2048,4480]{1,0:T(8,128)} %get-tuple-element.36, bf16[2048,4480]{1,0:T(8,128)(2,1)} %convolution_convert_fusion.4, f32[2048,4480]{1,0:T(8,128)} %fusion.23, bf16[1,2048,1280]{1,2,0:T(8,128)(2,1)} %copy.20, f32[2048]{0:T(1024)S(1)} %copy-done.16), kind=kOutput, calls=%fused_computation.22 | convolution fusion | flops 23602626560 | bytes 108470272 | tf_op jit(solution)/shard_map/dot_general | solution.py:10
  456.4 0.0 reduce-scatter.11.cloned.1.call-start
  456.5 37.7 %convolution_convert_fusion.1 = bf16[1280,4480]{1,0:T(8,128)(2,1)} fusion(bf16[2048,4480]{1,0:T(8,128)(2,1)} %convolution_convert_fusion.4, f32[2048,4480]{1,0:T(8,128)} %fusion.23, bf16[1,2048,1280]{1,2,0:T(8,128)(2,1)} %copy.20, f32[2048]{0:T(1024)S(1)} %copy-done.16), kind=kOutput, calls=%fused_computation.20 | convolution fusion | flops 23565926400 | bytes 71770112 | tf_op jit(solution)/shard_map/dot_general | solution.py:10
  494.2 0.0 reduce-scatter.13.cloned.1.call-start
  494.2 0.6 copy-done.12
  494.9 31.5 %convolution_convert_fusion = bf16[1280,4480]{1,0:T(8,128)(2,1)} fusion(bf16[2048,4480]{1,0:T(8,128)(2,1)} %get-tuple-element.10, bf16[2048,1280]{0,1:T(8,128)(2,1)} %get-tuple-element.38, f32[2048]{0:T(1024)S(1)} %copy-done.12), kind=kOutput, calls=%fused_computation.19 | convolution fusion | flops 23501701120 | bytes 35069952 | tf_op jit(solution)/shard_map/dot_general | solution.py:10
  526.3 0.0 reduce-scatter.15.cloned.1.call-start
  526.4 29.8 %convolution_convert_fusion.7 = bf16[4480,1280]{1,0:T(8,128)(2,1)} fusion(bf16[2048,4480]{1,0:T(8,128)(2,1)} %get-tuple-element.35, bf16[2048,1280]{0,1:T(8,128)(2,1)} %fusion.51), kind=kOutput, calls=%fused_computation.26 | convolution fusion | flops 23493836800 | bytes 35061760 | tf_op jit(solution)/shard_map/dot_general | solution.py:10
  556.2 0.0 reduce-scatter.17.cloned.1.call-start
  556.3 38.9 %convolution_convert_fusion.6 = bf16[4480,1280]{1,0:T(8,128)(2,1)} fusion(f32[2048,4480]{1,0:T(8,128)} %get-tuple-element.39, f32[2048,4480]{1,0:T(8,128)} %fusion.12, bf16[1,2048,1280]{2,1,0:T(8,128)(2,1)} %param.12), kind=kOutput, calls=%fused_computation.25 | convolution fusion | flops 23548887040 | bytes 90112000 | tf_op jit(solution)/shard_map/dot_general | solution.py:10
  595.2 0.0 all-gather.15.cloned.1.call-start
  595.2 16.3 %fusion.130 = (bf16[1,4480,1280]{2,1,0:T(8,128)(2,1)}, bf16[1,4480,1280]{2,1,0:T(8,128)(2,1)}) fusion(bf16[2,4480,1280]{2,1,0:T(8,128)(2,1)} %param.15), kind=kLoop, calls=%fused_computation.174 | loop fusion | bytes 45875200 | tf_op jit(solution)/shard_map/slice | solution.py:58
  611.5 2.7 fusion.73
  614.2 2.7 fusion.72
  618.2 2.7 fusion.74
  621.6 76.8 %reduce-scatter.13.cloned.1.call-done = bf16[160,4480]{1,0:T(8,128)(2,1)} async-done(((bf16[1280,4480]{1,0:T(8,128)(2,1)}), bf16[160,4480]{1,0:T(8,128)(2,1)}) %reduce-scatter.13.cloned.1.call-update) | async-done | bytes 1433616 | tf_op jit(solution)/shard_map/reduce_scatter | solution.py:52
  698.4 2.7 fusion.75
  701.7 77.7 %reduce-scatter.15.cloned.1.call-done = bf16[560,1280]{1,0:T(8,128)(2,1)} async-done(((bf16[4480,1280]{1,0:T(8,128)(2,1)}), bf16[560,1280]{1,0:T(8,128)(2,1)}) %reduce-scatter.15.cloned.1.call-update) | async-done | bytes 1433616 | tf_op jit(solution)/shard_map/reduce_scatter | solution.py:52
  779.5 2.7 fusion.76
  782.8 77.7 %reduce-scatter.17.cloned.1.call-done = bf16[560,1280]{1,0:T(8,128)(2,1)} async-done(((bf16[4480,1280]{1,0:T(8,128)(2,1)}), bf16[560,1280]{1,0:T(8,128)(2,1)}) %reduce-scatter.17.cloned.1.call-update) | async-done | bytes 1433616 | tf_op jit(solution)/shard_map/reduce_scatter | solution.py:52
  860.6 2.7 fusion.77
  863.9 22.5 %psum.7 = f32[]{:T(128)} all-reduce(f32[]{:T(128)S(6)} %add.172), channel_id=1, replica_groups=mesh['rep'=1,'dp'=8] {'dp'}, use_global_device_ids=true, to_apply=%region_15.16 | all-reduce | flops 1 | bytes 8 | tf_op jit(solution)/shard_map/psum | solution.py:75
  887.1 10.9 fusion.92
  898.0 0.0 all-gather.17.cloned.1.call-start
  898.1 0.7 all-gather.17.cloned.1.call-update
  898.8 8.8 fusion.131
  907.6 9.1 fusion.86
  916.8 0.5 all-gather.13.cloned.1.call-update
  917.4 8.8 fusion.132
  926.2 9.1 fusion.80
  935.4 0.0 all-gather.9.cloned.1.call-start
  935.4 0.5 all-gather.9.cloned.1.call-update
  936.0 9.0 pad_maximum_fusion.5
  945.0 0.9 copy-done.1
  945.9 0.9 copy-done.2
  946.8 0.8 copy-done.3
  947.6 6.0 pad_maximum_fusion.4
  953.7 1.4 copy-done.6
  955.1 0.8 copy-done.7
  955.9 4.7 pad_maximum_fusion.3
  960.6 1.0 all-gather.15.cloned.1.call-done
  961.6 63.4 %all-gather.17.cloned.1.call-done = bf16[4480,1280]{1,0:T(8,128)(2,1)} async-done(((bf16[560,1280]{1,0:T(8,128)(2,1)}), bf16[4480,1280]{1,0:T(8,128)(2,1)}) %all-gather.17.cloned.1.call-update) | async-done | bytes 11468816 | tf_op jit(solution)/shard_map/all_gather | solution.py:85
  1025.1 19.7 %pad_maximum_fusion.2 = bf16[2,4480,1280]{2,1,0:T(8,128)(2,1)} fusion(bf16[1,4480,1280]{2,1,0:T(8,128)(2,1)} %bitcast.197, bf16[1,4480,1280]{2,1,0:T(8,128)(2,1)} %bitcast.196), kind=kLoop, calls=%fused_computation.18 | loop fusion | flops 11468800 | bytes 45875200 | tf_op jit(solution)/shard_map/stack | solution.py:85
  1044.8 43.7 %all-gather.11.cloned.1.call-done = bf16[1280,4480]{1,0:T(8,128)(2,1)} async-done(((bf16[160,4480]{1,0:T(8,128)(2,1)}), bf16[1280,4480]{1,0:T(8,128)(2,1)}) %all-gather.11.cloned.1.call-update) | async-done | bytes 11468816 | tf_op jit(solution)/shard_map/all_gather | solution.py:85
  1088.5 63.3 %all-gather.13.cloned.1.call-done = bf16[1280,4480]{1,0:T(8,128)(2,1)} async-done(((bf16[160,4480]{1,0:T(8,128)(2,1)}), bf16[1280,4480]{1,0:T(8,128)(2,1)}) %all-gather.13.cloned.1.call-update) | async-done | bytes 11468816 | tf_op jit(solution)/shard_map/all_gather | solution.py:85
  1151.8 20.0 %pad_maximum_fusion.1 = bf16[2,1280,4480]{2,1,0:T(8,128)(2,1)} fusion(bf16[1,1280,4480]{2,1,0:T(8,128)(2,1)} %bitcast.199, bf16[1,1280,4480]{2,1,0:T(8,128)(2,1)} %bitcast.198), kind=kLoop, calls=%fused_computation.17 | loop fusion | flops 11468800 | bytes 45875200 | tf_op jit(solution)/shard_map/stack | solution.py:85
  1171.7 43.5 %all-gather.7.cloned.1.call-done = bf16[1280,4480]{1,0:T(8,128)(2,1)} async-done(((bf16[160,4480]{1,0:T(8,128)(2,1)}), bf16[1280,4480]{1,0:T(8,128)(2,1)}) %all-gather.7.cloned.1.call-update) | async-done | bytes 11468816 | tf_op jit(solution)/shard_map/all_gather | solution.py:85
  1215.2 63.3 %all-gather.9.cloned.1.call-done = bf16[1280,4480]{1,0:T(8,128)(2,1)} async-done(((bf16[160,4480]{1,0:T(8,128)(2,1)}), bf16[1280,4480]{1,0:T(8,128)(2,1)}) %all-gather.9.cloned.1.call-update) | async-done | bytes 11468816 | tf_op jit(solution)/shard_map/all_gather | solution.py:85
  1278.5 20.0 %pad_maximum_fusion = bf16[2,1280,4480]{2,1,0:T(8,128)(2,1)} fusion(bf16[1,1280,4480]{2,1,0:T(8,128)(2,1)} %bitcast.201, bf16[1,1280,4480]{2,1,0:T(8,128)(2,1)} %bitcast.200), kind=kLoop, calls=%fused_computation.16 | loop fusion | flops 11468800 | bytes 45875200 | tf_op jit(solution)/shard_map/stack | solution.py:85
  (47 shorter events, 0.4 us)
Async XLA Ops:
  7.2 604.3 %reduce-scatter.9.cloned.1.call-start = ((), (), s32[]{:S(2)}) async-start(), calls=%async_computation.7 | async-start | bytes 12902400 | tf_op jit(solution)/shard_map/reduce_scatter | solution.py:52
  18.7 31.6 %copy-start.15 = (f32[2048]{0:T(1024)}, f32[2048]{0:T(1024)S(1)}, u32[]{:S(2)}) copy-start(f32[2048]{0:T(1024)S(1)} %add_rsqrt_fusion.1) | copy-start | bytes 24580
  141.4 31.6 %copy-start.13 = (f32[2048]{0:T(1024)}, f32[2048]{0:T(1024)S(1)}, u32[]{:S(2)}) copy-start(f32[2048]{0:T(1024)S(1)} %get-tuple-element.37) | copy-start | bytes 24580
  141.4 227.1 %copy-start.11 = (f32[2048]{0:T(1024)}, f32[2048]{0:T(1024)S(1)}, u32[]{:S(2)}) copy-start(f32[2048]{0:T(1024)S(1)} %add_rsqrt_fusion) | copy-start | bytes 24580
  141.4 31.6 %copy-start.10 = (bf16[2048,1280]{0,1:T(8,128)(2,1)S(1)}, bf16[2048,1280]{0,1:T(8,128)(2,1)}, u32[]{:S(2)}) copy-start(bf16[2048,1280]{0,1:T(8,128)(2,1)} %get-tuple-element.38) | copy-start | bytes 15728644
  294.1 320.0 %reduce-scatter.7.cloned.1.call-start = ((), (), s32[]{:S(2)}) async-start(), calls=%async_computation.6 | async-start | bytes 12902400 | tf_op jit(solution)/shard_map/reduce_scatter | solution.py:52
  360.3 8.1 copy-start.14
  380.9 31.5 %copy-start.16 = (f32[2048]{0:T(1024)S(1)}, f32[2048]{0:T(1024)}, u32[]{:S(2)}) copy-start(f32[2048]{0:T(1024)} %copy-done.15) | copy-start | bytes 24580
  456.4 161.8 %reduce-scatter.11.cloned.1.call-start = ((), (), s32[]{:S(2)}) async-start(), calls=%async_computation.8 | async-start | bytes 12902400 | tf_op jit(solution)/shard_map/reduce_scatter | solution.py:52
  494.2 0.7 copy-start.12
  494.2 204.2 %reduce-scatter.13.cloned.1.call-start = ((), (), s32[]{:S(2)}) async-start(), calls=%async_computation.9 | async-start | bytes 12902400 | tf_op jit(solution)/shard_map/reduce_scatter | solution.py:52
  526.3 253.1 %reduce-scatter.15.cloned.1.call-start = ((), (), s32[]{:S(2)}) async-start(), calls=%async_computation.10 | async-start | bytes 12902400 | tf_op jit(solution)/shard_map/reduce_scatter | solution.py:52
  556.2 304.3 %reduce-scatter.17.cloned.1.call-start = ((), (), s32[]{:S(2)}) async-start(), calls=%async_computation.11 | async-start | bytes 12902400 | tf_op jit(solution)/shard_map/reduce_scatter | solution.py:52
  595.2 366.5 %all-gather.15.cloned.1.call-start = ((), (), s32[]{:S(2)}) async-start(), calls=%async_computation.16 | async-start | bytes 12902400 | tf_op jit(solution)/shard_map/all_gather | solution.py:85
  898.0 127.1 %all-gather.17.cloned.1.call-start = ((), (), s32[]{:S(2)}) async-start(), calls=%async_computation.17 | async-start | bytes 12902400 | tf_op jit(solution)/shard_map/all_gather | solution.py:85
  898.8 189.7 %all-gather.11.cloned.1.call-start = ((), (), s32[]{:S(2)}) async-start(), calls=%async_computation.14 | async-start | bytes 12902400 | tf_op jit(solution)/shard_map/all_gather | solution.py:85
  898.8 8.8 copy-start.9
  916.7 235.0 %all-gather.13.cloned.1.call-start = ((), (), s32[]{:S(2)}) async-start(), calls=%async_computation.15 | async-start | bytes 12902400 | tf_op jit(solution)/shard_map/all_gather | solution.py:85
  917.3 8.9 copy-start.8
  917.3 297.8 %all-gather.7.cloned.1.call-start = ((), (), s32[]{:S(2)}) async-start(), calls=%async_computation.12 | async-start | bytes 12902400 | tf_op jit(solution)/shard_map/all_gather | solution.py:85
  935.4 343.1 %all-gather.9.cloned.1.call-start = ((), (), s32[]{:S(2)}) async-start(), calls=%async_computation.13 | async-start | bytes 12902400 | tf_op jit(solution)/shard_map/all_gather | solution.py:85
  936.0 9.0 copy-start
  936.0 10.0 copy-start.1
  936.0 10.8 copy-start.2
  936.0 11.6 copy-start.3
  947.6 6.1 copy-start.4
  947.6 6.1 copy-start.5
  947.6 7.5 copy-start.6
  947.6 8.3 copy-start.7
Sparse Core Ops, SparseCore 0:
  294.3 80.0 reduce-scatter.8
  456.6 80.0 reduce-scatter.6
  540.1 77.1 reduce-scatter.10
  621.2 77.1 reduce-scatter.12
  702.2 77.1 reduce-scatter.14
  783.3 77.1 reduce-scatter.16
  898.1 63.4 all-gather.14
  963.5 61.5 all-gather.16
  1026.9 61.5 all-gather.10
  1090.2 61.5 all-gather.12
  1153.6 61.5 all-gather.6
  1216.9 61.5 all-gather.8
